TPU v7x, 32 devices: a whole 2x2x4 slice. The times are simulated.
32 devices in a mesh: traj: 16 (over z, y, core), tm: 2 (over x).
Axes of the slice: x: 2, y: 2, z: 4, core: 2. Of those that a mesh axis runs over, the one named last changes fastest.
Arguments:
- states: float32 [2, 32, 4096], P('tm', None, 'traj'), may hold values from -6 to 6
- vectors: bfloat16 [64, 4096], P(None, 'traj'), may hold values from -6 to 6
- kernel_scale: float32 [2], P('tm'), may hold values from 6 to 16
- neighbour_blocks: int32 [32, 24], P('traj'), may hold values from 0 to 31, as said below
- neighbour_count: int32 [32], P('traj'), may hold values from 6 to 24, as said below
Outputs:
- result: float32 [64, 4096], P(None, 'traj')
Inputs may be any that keep to these rules, and one draw needn't show every extreme that they name: `neighbour_blocks`: row b names 24 different blocks, the first of them b itself. Only the first neighbour_count[b] entries of row b of neighbour_blocks are neighbours of block b; some block uses all 24.
All inputs are finite; a program needn't handle non-finite values.
Results may differ from a plain program's by a relative error of at most 0.0013.
Values may be sent and summed in bfloat16 or wider, within the bound.
No kernel may reach another device: no remote copies, remote signals or barrier semaphores. Data moves between devices by JAX's collectives and lax.ppermute only.
A program may use at most 64 MiB of HBM per device.

v0:
```python
import math
import jax
import jax.numpy as jnp
from jax import lax
from jax.sharding import PartitionSpec as P

BLK = 128


def linked_blocks(neighbour_blocks, neighbour_count, blocks_total):
    slots = neighbour_blocks.shape[1]
    named = neighbour_blocks[:, :, None] == jnp.arange(blocks_total, dtype=jnp.int32)[None, None, :]
    within = jnp.arange(slots, dtype=jnp.int32)[None, :, None] < neighbour_count[:, None, None]
    return jnp.any(named & within, axis=1).astype(jnp.float32)


def per_device(states, vectors, kernel_scale, neighbour_blocks, neighbour_count):
    coords_all = lax.all_gather(states, "traj", axis=2, tiled=True)[0]
    vectors_all = lax.all_gather(vectors, "traj", axis=1, tiled=True)
    own = states[0]
    spread = kernel_scale[0]
    own_rows = own.shape[1]
    columns = coords_all.shape[1]
    vector_count = vectors.shape[0]
    blocks_total = columns // BLK
    block_rows = own_rows // BLK
    own_squares = jnp.sum(own * own, axis=0)
    all_squares = jnp.sum(coords_all * coords_all, axis=0)
    tile_width = math.gcd(columns, 512)
    tile_count = columns // tile_width
    linked = linked_blocks(neighbour_blocks, neighbour_count, blocks_total)

    def dense_kernel(tile_index):
        offset = tile_index * tile_width
        slab = lax.dynamic_slice_in_dim(coords_all, offset, tile_width, 1)
        cross = lax.dot_general(
            own, slab, (((0,), (0,)), ((), ())), precision=lax.Precision.HIGHEST
        )
        slab_squares = lax.dynamic_slice_in_dim(all_squares, offset, tile_width, 0)
        distance = own_squares[:, None] + slab_squares[None, :] - 2.0 * cross
        mask = lax.dynamic_slice_in_dim(linked, offset // BLK, tile_width // BLK, 1)
        shaped = jnp.exp(-distance / spread).reshape(block_rows, BLK, tile_width // BLK, BLK)
        return (mask[:, None, :, None] * shaped).reshape(own_rows, tile_width)

    def first_dense(tile_index, carry):
        row_sum, pushed = carry
        kernel = dense_kernel(tile_index)
        weights = kernel.astype(jnp.bfloat16)
        slab_vectors = lax.dynamic_slice_in_dim(vectors_all, tile_index * tile_width, tile_width, 1)
        pushed = pushed + lax.dot_general(
            slab_vectors, weights, (((1,), (1,)), ((), ())), preferred_element_type=jnp.float32
        )
        return (row_sum + jnp.sum(kernel, axis=1), pushed)

    row_sum, pushed = lax.fori_loop(
        0,
        tile_count,
        first_dense,
        (jnp.zeros((own_rows,), jnp.float32), jnp.zeros((vector_count, own_rows), jnp.float32)),
    )
    scaled = (pushed / (row_sum * row_sum)[None, :]).astype(jnp.bfloat16)
    lists_whole, counts_whole = (
        lax.all_gather(neighbour_blocks, "traj", axis=0, tiled=True),
        lax.all_gather(neighbour_count, "traj", axis=0, tiled=True),
    )
    linked_whole = linked_blocks(lists_whole, counts_whole, blocks_total)
    own_start = lax.axis_index("traj") * block_rows
    column_mask = lax.dynamic_slice_in_dim(linked_whole, own_start, block_rows, 1)
    scaled_whole = lax.all_gather(scaled, "traj", axis=1, tiled=True)

    def pull_tile(tile_index, total):
        offset = tile_index * tile_width
        slab = lax.dynamic_slice_in_dim(coords_all, offset, tile_width, 1)
        cross = lax.dot_general(
            slab, own, (((0,), (0,)), ((), ())), precision=lax.Precision.HIGHEST
        )
        slab_squares = lax.dynamic_slice_in_dim(all_squares, offset, tile_width, 0)
        distance = slab_squares[:, None] + own_squares[None, :] - 2.0 * cross
        mask = lax.dynamic_slice_in_dim(column_mask, offset // BLK, tile_width // BLK, 0)
        shaped = jnp.exp(-distance / spread).reshape(tile_width // BLK, BLK, block_rows, BLK)
        weights = (
            (mask[:, None, :, None] * shaped).reshape(tile_width, own_rows).astype(jnp.bfloat16)
        )
        slab_scaled = lax.dynamic_slice_in_dim(scaled_whole, offset, tile_width, 1)
        return total + jnp.dot(slab_scaled, weights, preferred_element_type=jnp.float32)

    own_pulled = lax.fori_loop(
        0, tile_count, pull_tile, jnp.zeros((vector_count, own_rows), jnp.float32)
    )
    result = lax.psum(own_pulled, "tm")
    return result


def solution(mesh):
    in_specs = (P("tm", None, "traj"), P(None, "traj"), P("tm"), P("traj", None), P("traj"))
    out_specs = P(None, "traj")
    return jax.shard_map(
        per_device, mesh=mesh, in_specs=in_specs, out_specs=out_specs, check_vma=False
    )
```

profile of v0, /device:TPU:0, one launch (start us, length us, event | category | flops | bytes accessed | tf_op | source)
XLA Modules:
  0.0 164.4 jit_solution(14845167993915511679)
XLA Ops:
  6.5 24.9 %all_gather.15 = f32[1,32,4096]{2,1,0:T(8,128)S(1)} all-gather(f32[1,32,256]{2,1,0:T(8,128)} %param.9), channel_id=1, replica_groups=mesh['traj'=16,'tm'=2] {'traj'}, dimensions={2}, use_global_device_ids=true | all-gather | bytes 557056 | tf_op jit(solution)/shard_map/all_gather | solution.py:18
  32.3 19.0 %all_gather.16 = bf16[64,4096]{1,0:T(8,128)(2,1)S(1)} all-gather(bf16[64,256]{1,0:T(8,128)(2,1)S(1)} %copy-done.2), channel_id=1, replica_groups=mesh['traj'=16,'tm'=2] {'traj'}, dimensions={1}, use_global_device_ids=true | all-gather | bytes 557056 | tf_op jit(solution)/shard_map/all_gather | solution.py:19
  52.1 17.0 %while.34 = (s32[]{:T(128)}, f32[256]{0:T(256)S(1)}, f32[64,256]{1,0:T(8,128)S(1)}, f32[2,32]{1,0:T(2,128)S(1)}, f32[256]{0:T(256)S(1)}, /*index=5*/f32[4096]{0:...) while((s32[]{:T(128)}, f32[256]{0:T(256)S(1)}, ...), condition=%wide.region_6.7_spmd.clone, body=%wide.region_4.0_spmd.clone.sunk | while | flops 68190488 | bytes 1879617 | solution.py:55
  52.6 1.4 fusion.42
  54.7 1.4 fusion.42
  56.8 1.4 fusion.42
  59.0 1.4 fusion.42
  61.1 1.4 fusion.42
  63.2 1.4 fusion.42
  65.4 1.4 fusion.42
  67.5 1.4 fusion.42
  69.1 20.3 %all_gather.17 = bf16[64,4096]{1,0:T(8,128)(2,1)S(1)} all-gather(bf16[64,256]{1,0:T(8,128)(2,1)S(1)} %divide_convert_fusion), channel_id=1, replica_groups=mesh['traj'=16,'tm'=2] {'traj'}, dimensions={1}, use_global_device_ids=true | all-gather | bytes 557056 | tf_op jit(solution)/shard_map/all_gather | solution.py:69
  91.7 8.0 %all-reduce = s32[32]{0:T(128)S(1)} all-reduce(s32[32]{0:T(128)S(1)} %dynamic-update-slice), channel_id=1, replica_groups=mesh['traj'=16,'tm'=2] {'traj'}, use_global_device_ids=true, to_apply=%add | all-reduce | flops 32 | bytes 256
  99.8 21.6 %all-gather = s32[16,2,24]{2,1,0:T(2,128)S(1)} all-gather(s32[1,2,24]{2,1,0:T(2,128)S(1)} %bitcast.53), channel_id=1, replica_groups=mesh['traj'=16,'tm'=2] {'traj'}, dimensions={0}, use_global_device_ids=true | all-gather | bytes 3264 | tf_op jit(solution)/shard_map/all_gather | solution.py:63
  121.7 15.4 %while.35 = (s32[]{:T(128)}, f32[64,256]{1,0:T(8,128)S(1)}, bf16[64,4096]{1,0:T(8,128)(2,1)S(1)}, f32[32,2]{1,0:T(8,128)S(1)}, f32[4096]{0:T(1024)S(1)}, /*index...) while((s32[]{:T(128)}, f32[64,256]{1,0:T(8,128)S(1)}, ...), condition=%wide.region_8.9_spmd.clone, body=%wide.region_7.8_spmd.clone.sunk | while | flops 68059160 | bytes 1875448 | solution.py:87
  122.0 1.4 fusion.47
  124.0 1.4 fusion.47
  125.9 1.4 fusion.47
  129.8 1.4 fusion.47
  131.7 1.4 fusion.47
  133.6 1.4 fusion.47
  135.5 1.4 fusion.47
  137.8 18.3 %all-reduce.3.cloned.1.call-done = f32[64,256]{1,0:T(8,128)} async-done(((f32[64,256]{1,0:T(8,128)}), f32[64,256]{1,0:T(8,128)}) %all-reduce.3.cloned.1.call-update) | async-done | bytes 65552 | tf_op jit(solution)/shard_map/psum | solution.py:90
  156.1 1.5 copy.35
  (111 shorter events, 14.7 us)
Async XLA Ops:
  6.5 24.9 %copy-start.1 = (f32[1,32,256]{2,1,0:T(8,128)S(1)}, f32[1,32,256]{2,1,0:T(8,128)}, u32[]{:S(2)}) copy-start(f32[1,32,256]{2,1,0:T(8,128)} %param.9) | copy-start | bytes 98308
  6.5 149.6 %all-reduce.3.cloned.1.call-start = ((), (), s32[]{:S(2)}) async-start(), calls=%async_computation | async-start | bytes 131072 | tf_op jit(solution)/shard_map/psum | solution.py:90
  31.5 0.8 copy-start.2
  32.3 19.0 %copy-start.4 = (s32[2]{0:T(128)S(1)}, s32[2]{0:T(128)}, u32[]{:S(2)}) copy-start(s32[2]{0:T(128)} %param.13) | copy-start | bytes 28
  51.3 0.7 copy-start.3
  89.5 0.7 copy-start.5
  137.1 0.6 copy-start
Sparse Core Ops, SparseCore 0:
  137.9 18.1 all-reduce.2
where the time goes:
time: 165 us; the launch traced here: 164 us
  blocking collectives  93.8 us (57%)
  matrix products  25.1 us (15%)
  waiting for transfers between devices  18.4 us (11%)
  between operations  14.2 us (9%)
  local copies, waits for them, and re-layouts  10.9 us (7%)
    all_gather x1, blocking collectives, per_device(): coords_all = lax.all_gather(states, 'traj', axis=2, tiled=True)[0]  24.9 us
    all_gather x1, blocking collectives, per_device(): lax.all_gather(neighbour_blocks, 'traj', axis=0, tiled=True)  21.6 us
    all_gather x1, blocking collectives, per_device(): scaled_whole = lax.all_gather(scaled, 'traj', axis=1, tiled=True)  20.3 us
    all_gather x1, blocking collectives, per_device(): vectors_all = lax.all_gather(vectors, 'traj', axis=1, tiled=True)  19 us
    psum x1, waiting for transfers between devices, per_device(): result = lax.psum(own_pulled, 'tm')  18.3 us
    dot_general x8, matrix products, dense_kernel(): lax.dot_general(own, slab, (((0,), (0,)), ((), ())), precision=lax.Precis...  11.2 us
    dot_general x8, matrix products, pull_tile(): lax.dot_general(slab, own, (((0,), (0,)), ((), ())), precision=lax.Precis...  10.9 us
    unnamed x1, blocking collectives  7.97 us
  transfers between devices with their start and end apart: 1, of which 1 were waited for; matrix products, arithmetic and copies ran while one was open for 0% of the time, Pallas kernels for 0%

commit v1 on v0

--- a/solution.py
+++ b/solution.py
@@ -66,7 +66,12 @@
     linked_whole = linked_blocks(lists_whole, counts_whole, blocks_total)
     own_start = lax.axis_index("traj") * block_rows
     column_mask = lax.dynamic_slice_in_dim(linked_whole, own_start, block_rows, 1)
-    scaled_whole = lax.all_gather(scaled, "traj", axis=1, tiled=True)
+    ring = [scaled]
+    for hop in range(15):
+        ring.append(lax.ppermute(ring[-1], "traj", [(dev, (dev + 1) % 16) for dev in range(16)]))
+    scaled_whole = jnp.roll(
+        jnp.concatenate(ring[::-1], axis=1), (lax.axis_index("traj") + 1) * ring[0].shape[1], axis=1
+    )
 
     def pull_tile(tile_index, total):
         offset = tile_index * tile_width

time: 165 us -> 224 us (1.36)
  waiting for transfers between devices: 18.4 us -> 95.9 us
  blocking collectives: 93.8 us -> 74 us
    ppermute x0 -> x15, waiting for transfers between devices: none -> 77.6 us  [per_device(): lax.ppermute(ring[-1], 'traj', [(dev, (dev + 1) % 16) for dev in range(16)])]
    all_gather x1 -> x0, blocking collectives: 20.3 us -> none  [per_device(): scaled_whole = lax.all_gather(scaled, 'traj', axis=1, tiled=True)]
    unnamed x1, blocking collectives: 7.97 us -> 12.1 us
    all_gather x1, blocking collectives: 21.6 us -> 18 us  [per_device(): lax.all_gather(neighbour_blocks, 'traj', axis=0, tiled=True)]
    unnamed x16 -> x46, local copies, waits for them, and re-layouts: 4.95 us -> 5.01 us
  transfers between devices with their start and end apart: 1 -> 16, of which waited for: 1 -> 14; matrix products, arithmetic and copies ran while one was open for 0% -> 1% of each run, Pallas kernels for 0% -> 0%
where the time goes in v1:
time: 224 us; the launch traced here: 223 us
  waiting for transfers between devices  95.9 us (43%)
  blocking collectives  74 us (33%)
  matrix products  25.1 us (11%)
  between operations  14.4 us (6%)
  local copies, waits for them, and re-layouts  11 us (5%)
    ppermute x15, waiting for transfers between devices, per_device(): lax.ppermute(ring[-1], 'traj', [(dev, (dev + 1) % 16) for dev in range(16)])  77.6 us
    all_gather x1, blocking collectives, per_device(): coords_all = lax.all_gather(states, 'traj', axis=2, tiled=True)[0]  24.9 us
    all_gather x1, blocking collectives, per_device(): vectors_all = lax.all_gather(vectors, 'traj', axis=1, tiled=True)  19 us
    psum x1, waiting for transfers between devices, per_device(): result = lax.psum(own_pulled, 'tm')  18.4 us
    all_gather x1, blocking collectives, per_device(): lax.all_gather(neighbour_blocks, 'traj', axis=0, tiled=True)  18 us
    unnamed x1, blocking collectives  12.1 us
    dot_general x8, matrix products, dense_kernel(): lax.dot_general(own, slab, (((0,), (0,)), ((), ())), precision=lax.Precis...  11.2 us
    dot_general x8, matrix products, pull_tile(): lax.dot_general(slab, own, (((0,), (0,)), ((), ())), precision=lax.Precis...  10.9 us
  transfers between devices with their start and end apart: 16, of which 14 were waited for; matrix products, arithmetic and copies ran while one was open for 1% of the time, Pallas kernels for 0%

profile of v1, /device:TPU:0, one launch (start us, length us, event | category | flops | bytes accessed | tf_op | source)
XLA Modules:
  0.0 223.2 jit_solution(12753077875305303366)
XLA Ops:
  6.5 24.9 %all_gather.12 = f32[1,32,4096]{2,1,0:T(8,128)S(1)} all-gather(f32[1,32,256]{2,1,0:T(8,128)} %param.9), channel_id=1, replica_groups=mesh['traj'=16,'tm'=2] {'traj'}, dimensions={2}, use_global_device_ids=true | all-gather | bytes 557056 | tf_op jit(solution)/shard_map/all_gather | solution.py:18
  32.3 19.0 %all_gather.13 = bf16[64,4096]{1,0:T(8,128)(2,1)S(1)} all-gather(bf16[64,256]{1,0:T(8,128)(2,1)S(1)} %copy-done.2), channel_id=1, replica_groups=mesh['traj'=16,'tm'=2] {'traj'}, dimensions={1}, use_global_device_ids=true | all-gather | bytes 557056 | tf_op jit(solution)/shard_map/all_gather | solution.py:19
  52.1 17.0 %while.34 = (s32[]{:T(128)}, f32[256]{0:T(256)S(1)}, f32[64,256]{1,0:T(8,128)S(1)}, f32[2,32]{1,0:T(2,128)S(1)}, f32[256]{0:T(256)S(1)}, /*index=5*/f32[4096]{0:...) while((s32[]{:T(128)}, f32[256]{0:T(256)S(1)}, ...), condition=%wide.region_6.7_spmd.clone, body=%wide.region_4.0_spmd.clone.sunk | while | flops 68190488 | bytes 1879617 | solution.py:55
  52.6 1.4 fusion.42
  54.7 1.4 fusion.42
  63.2 1.4 fusion.42
  69.5 5.7 %collective-permute-done = bf16[64,256]{1,0:T(8,128)(2,1)S(1)} collective-permute-done((bf16[64,256]{1,0:T(8,128)(2,1)S(1)}, bf16[64,256]{1,0:T(8,128)(2,1)S(1)}, u32[]{:S(2)}, u32[]{:S(2)}) %collective-permute-start) | collective-permute-done | bytes 32800 | tf_op jit(solution)/shard_map/ppermute | solution.py:71
  75.2 6.0 %collective-permute-done.1 = bf16[64,256]{1,0:T(8,128)(2,1)S(1)} collective-permute-done((bf16[64,256]{1,0:T(8,128)(2,1)S(1)}, bf16[64,256]{1,0:T(8,128)(2,1)S(1)}, u32[]{:S(2)}, u32[]{:S(2)}) %collective-permute-start.1) | collective-permute-done | bytes 32800 | tf_op jit(solution)/shard_map/ppermute | solution.py:71
  81.3 6.0 %collective-permute-done.2 = bf16[64,256]{1,0:T(8,128)(2,1)S(1)} collective-permute-done((bf16[64,256]{1,0:T(8,128)(2,1)S(1)}, bf16[64,256]{1,0:T(8,128)(2,1)S(1)}, u32[]{:S(2)}, u32[]{:S(2)}) %collective-permute-start.2) | collective-permute-done | bytes 32800 | tf_op jit(solution)/shard_map/ppermute | solution.py:71
  87.3 6.0 %collective-permute-done.3 = bf16[64,256]{1,0:T(8,128)(2,1)S(1)} collective-permute-done((bf16[64,256]{1,0:T(8,128)(2,1)S(1)}, bf16[64,256]{1,0:T(8,128)(2,1)S(1)}, u32[]{:S(2)}, u32[]{:S(2)}) %collective-permute-start.3) | collective-permute-done | bytes 32800 | tf_op jit(solution)/shard_map/ppermute | solution.py:71
  93.3 6.0 %collective-permute-done.4 = bf16[64,256]{1,0:T(8,128)(2,1)S(1)} collective-permute-done((bf16[64,256]{1,0:T(8,128)(2,1)S(1)}, bf16[64,256]{1,0:T(8,128)(2,1)S(1)}, u32[]{:S(2)}, u32[]{:S(2)}) %collective-permute-start.4) | collective-permute-done | bytes 32800 | tf_op jit(solution)/shard_map/ppermute | solution.py:71
  99.4 6.0 %collective-permute-done.5 = bf16[64,256]{1,0:T(8,128)(2,1)S(1)} collective-permute-done((bf16[64,256]{1,0:T(8,128)(2,1)S(1)}, bf16[64,256]{1,0:T(8,128)(2,1)S(1)}, u32[]{:S(2)}, u32[]{:S(2)}) %collective-permute-start.5) | collective-permute-done | bytes 32800 | tf_op jit(solution)/shard_map/ppermute | solution.py:71
  105.4 6.0 %collective-permute-done.6 = bf16[64,256]{1,0:T(8,128)(2,1)S(1)} collective-permute-done((bf16[64,256]{1,0:T(8,128)(2,1)S(1)}, bf16[64,256]{1,0:T(8,128)(2,1)S(1)}, u32[]{:S(2)}, u32[]{:S(2)}) %collective-permute-start.6) | collective-permute-done | bytes 32800 | tf_op jit(solution)/shard_map/ppermute | solution.py:71
  111.4 6.0 %collective-permute-done.7 = bf16[64,256]{1,0:T(8,128)(2,1)S(1)} collective-permute-done((bf16[64,256]{1,0:T(8,128)(2,1)S(1)}, bf16[64,256]{1,0:T(8,128)(2,1)S(1)}, u32[]{:S(2)}, u32[]{:S(2)}) %collective-permute-start.7) | collective-permute-done | bytes 32800 | tf_op jit(solution)/shard_map/ppermute | solution.py:71
  117.5 6.0 %collective-permute-done.8 = bf16[64,256]{1,0:T(8,128)(2,1)S(1)} collective-permute-done((bf16[64,256]{1,0:T(8,128)(2,1)S(1)}, bf16[64,256]{1,0:T(8,128)(2,1)S(1)}, u32[]{:S(2)}, u32[]{:S(2)}) %collective-permute-start.8) | collective-permute-done | bytes 32800 | tf_op jit(solution)/shard_map/ppermute | solution.py:71
  123.5 6.0 %collective-permute-done.9 = bf16[64,256]{1,0:T(8,128)(2,1)S(1)} collective-permute-done((bf16[64,256]{1,0:T(8,128)(2,1)S(1)}, bf16[64,256]{1,0:T(8,128)(2,1)S(1)}, u32[]{:S(2)}, u32[]{:S(2)}) %collective-permute-start.9) | collective-permute-done | bytes 32800 | tf_op jit(solution)/shard_map/ppermute | solution.py:71
  129.6 6.0 %collective-permute-done.10 = bf16[64,256]{1,0:T(8,128)(2,1)S(1)} collective-permute-done((bf16[64,256]{1,0:T(8,128)(2,1)S(1)}, bf16[64,256]{1,0:T(8,128)(2,1)S(1)}, u32[]{:S(2)}, u32[]{:S(2)}) %collective-permute-start.10) | collective-permute-done | bytes 32800 | tf_op jit(solution)/shard_map/ppermute | solution.py:71
  137.7 12.1 %all-reduce = s32[32]{0:T(128)S(1)} all-reduce(s32[32]{0:T(128)S(1)} %dynamic-update-slice), channel_id=1, replica_groups=mesh['traj'=16,'tm'=2] {'traj'}, use_global_device_ids=true, to_apply=%add | all-reduce | flops 32 | bytes 256
  149.9 18.0 %all-gather = s32[16,2,24]{2,1,0:T(2,128)S(1)} all-gather(s32[1,2,24]{2,1,0:T(2,128)S(1)} %bitcast.53), channel_id=1, replica_groups=mesh['traj'=16,'tm'=2] {'traj'}, dimensions={0}, use_global_device_ids=true | all-gather | bytes 3264 | tf_op jit(solution)/shard_map/all_gather | solution.py:63
  168.4 5.6 %collective-permute-done.13 = bf16[64,256]{1,0:T(8,128)(2,1)S(1)} collective-permute-done((bf16[64,256]{1,0:T(8,128)(2,1)S(1)}, bf16[64,256]{1,0:T(8,128)(2,1)S(1)}, u32[]{:S(2)}, u32[]{:S(2)}) %collective-permute-start.13) | collective-permute-done | bytes 32800 | tf_op jit(solution)/shard_map/ppermute | solution.py:71
  174.0 6.0 %collective-permute-done.14 = bf16[64,256]{1,0:T(8,128)(2,1)S(1)} collective-permute-done((bf16[64,256]{1,0:T(8,128)(2,1)S(1)}, bf16[64,256]{1,0:T(8,128)(2,1)S(1)}, u32[]{:S(2)}, u32[]{:S(2)}) %collective-permute-start.14) | collective-permute-done | bytes 32800 | tf_op jit(solution)/shard_map/ppermute | solution.py:71
  180.4 15.4 %while.35 = (s32[]{:T(128)}, f32[64,256]{1,0:T(8,128)S(1)}, bf16[64,4096]{1,0:T(8,128)(2,1)S(1)}, f32[32,2]{1,0:T(8,128)S(1)}, f32[4096]{0:T(1024)S(1)}, /*index...) while((s32[]{:T(128)}, f32[64,256]{1,0:T(8,128)S(1)}, ...), condition=%wide.region_8.9_spmd.clone, body=%wide.region_7.8_spmd.clone.sunk | while | flops 68059160 | bytes 1875448 | solution.py:92
  196.5 18.4 %all-reduce.3.cloned.1.call-done = f32[64,256]{1,0:T(8,128)} async-done(((f32[64,256]{1,0:T(8,128)}), f32[64,256]{1,0:T(8,128)}) %all-reduce.3.cloned.1.call-update) | async-done | bytes 65552 | tf_op jit(solution)/shard_map/psum | solution.py:95
  214.9 1.5 copy.66
  (173 shorter events, 31.9 us)
Async XLA Ops:
  6.5 24.9 %copy-start.1 = (f32[1,32,256]{2,1,0:T(8,128)S(1)}, f32[1,32,256]{2,1,0:T(8,128)}, u32[]{:S(2)}) copy-start(f32[1,32,256]{2,1,0:T(8,128)} %param.9) | copy-start | bytes 98308
  6.5 208.4 %all-reduce.3.cloned.1.call-start = ((), (), s32[]{:S(2)}) async-start(), calls=%async_computation | async-start | bytes 131072 | tf_op jit(solution)/shard_map/psum | solution.py:95
  31.5 0.8 copy-start.2
  32.3 19.0 %copy-start.4 = (s32[2]{0:T(128)S(1)}, s32[2]{0:T(128)}, u32[]{:S(2)}) copy-start(s32[2]{0:T(128)} %param.13) | copy-start | bytes 28
  51.3 0.7 copy-start.3
  69.1 6.1 %collective-permute-start = (bf16[64,256]{1,0:T(8,128)(2,1)S(1)}, bf16[64,256]{1,0:T(8,128)(2,1)S(1)}, u32[]{:S(2)}, u32[]{:S(2)}) collective-permute-start(bf16[64,256]{1,0:T(8,128)(2,1)S(1)} %divide_convert_fusion), channel_id=1, source_target_pairs={{0,2},{2,4},{4,6},{6,8},{8,10},{10,12},{12,14},{14,16},{16,18},{18... | collective-permute-start | bytes 98312 | tf_op jit(solution)/shard_map/ppermute | solution.py:71
  75.2 6.0 %collective-permute-start.1 = (bf16[64,256]{1,0:T(8,128)(2,1)S(1)}, bf16[64,256]{1,0:T(8,128)(2,1)S(1)}, u32[]{:S(2)}, u32[]{:S(2)}) collective-permute-start(bf16[64,256]{1,0:T(8,128)(2,1)S(1)} %collective-permute-done), channel_id=1, source_target_pairs={{0,2},{2,4},{4,6},{6,8},{8,10},{10,12},{12,14},{14,16},{16,18},{18... | collective-permute-start | bytes 98312 | tf_op jit(solution)/shard_map/ppermute | solution.py:71
  81.2 6.0 %collective-permute-start.2 = (bf16[64,256]{1,0:T(8,128)(2,1)S(1)}, bf16[64,256]{1,0:T(8,128)(2,1)S(1)}, u32[]{:S(2)}, u32[]{:S(2)}) collective-permute-start(bf16[64,256]{1,0:T(8,128)(2,1)S(1)} %collective-permute-done.1), channel_id=1, source_target_pairs={{0,2},{2,4},{4,6},{6,8},{8,10},{10,12},{12,14},{14,16},{16,18},{18... | collective-permute-start | bytes 98312 | tf_op jit(solution)/shard_map/ppermute | solution.py:71
  87.3 6.0 %collective-permute-start.3 = (bf16[64,256]{1,0:T(8,128)(2,1)S(1)}, bf16[64,256]{1,0:T(8,128)(2,1)S(1)}, u32[]{:S(2)}, u32[]{:S(2)}) collective-permute-start(bf16[64,256]{1,0:T(8,128)(2,1)S(1)} %collective-permute-done.2), channel_id=1, source_target_pairs={{0,2},{2,4},{4,6},{6,8},{8,10},{10,12},{12,14},{14,16},{16,18},{18... | collective-permute-start | bytes 98312 | tf_op jit(solution)/shard_map/ppermute | solution.py:71
  93.3 6.0 %collective-permute-start.4 = (bf16[64,256]{1,0:T(8,128)(2,1)S(1)}, bf16[64,256]{1,0:T(8,128)(2,1)S(1)}, u32[]{:S(2)}, u32[]{:S(2)}) collective-permute-start(bf16[64,256]{1,0:T(8,128)(2,1)S(1)} %collective-permute-done.3), channel_id=1, source_target_pairs={{0,2},{2,4},{4,6},{6,8},{8,10},{10,12},{12,14},{14,16},{16,18},{18... | collective-permute-start | bytes 98312 | tf_op jit(solution)/shard_map/ppermute | solution.py:71
  99.4 6.0 %collective-permute-start.5 = (bf16[64,256]{1,0:T(8,128)(2,1)S(1)}, bf16[64,256]{1,0:T(8,128)(2,1)S(1)}, u32[]{:S(2)}, u32[]{:S(2)}) collective-permute-start(bf16[64,256]{1,0:T(8,128)(2,1)S(1)} %collective-permute-done.4), channel_id=1, source_target_pairs={{0,2},{2,4},{4,6},{6,8},{8,10},{10,12},{12,14},{14,16},{16,18},{18... | collective-permute-start | bytes 98312 | tf_op jit(solution)/shard_map/ppermute | solution.py:71
  105.4 6.0 %collective-permute-start.6 = (bf16[64,256]{1,0:T(8,128)(2,1)S(1)}, bf16[64,256]{1,0:T(8,128)(2,1)S(1)}, u32[]{:S(2)}, u32[]{:S(2)}) collective-permute-start(bf16[64,256]{1,0:T(8,128)(2,1)S(1)} %collective-permute-done.5), channel_id=1, source_target_pairs={{0,2},{2,4},{4,6},{6,8},{8,10},{10,12},{12,14},{14,16},{16,18},{18... | collective-permute-start | bytes 98312 | tf_op jit(solution)/shard_map/ppermute | solution.py:71
  111.4 6.0 %collective-permute-start.7 = (bf16[64,256]{1,0:T(8,128)(2,1)S(1)}, bf16[64,256]{1,0:T(8,128)(2,1)S(1)}, u32[]{:S(2)}, u32[]{:S(2)}) collective-permute-start(bf16[64,256]{1,0:T(8,128)(2,1)S(1)} %collective-permute-done.6), channel_id=1, source_target_pairs={{0,2},{2,4},{4,6},{6,8},{8,10},{10,12},{12,14},{14,16},{16,18},{18... | collective-permute-start | bytes 98312 | tf_op jit(solution)/shard_map/ppermute | solution.py:71
  117.5 6.0 %collective-permute-start.8 = (bf16[64,256]{1,0:T(8,128)(2,1)S(1)}, bf16[64,256]{1,0:T(8,128)(2,1)S(1)}, u32[]{:S(2)}, u32[]{:S(2)}) collective-permute-start(bf16[64,256]{1,0:T(8,128)(2,1)S(1)} %collective-permute-done.7), channel_id=1, source_target_pairs={{0,2},{2,4},{4,6},{6,8},{8,10},{10,12},{12,14},{14,16},{16,18},{18... | collective-permute-start | bytes 98312 | tf_op jit(solution)/shard_map/ppermute | solution.py:71
  123.5 6.0 %collective-permute-start.9 = (bf16[64,256]{1,0:T(8,128)(2,1)S(1)}, bf16[64,256]{1,0:T(8,128)(2,1)S(1)}, u32[]{:S(2)}, u32[]{:S(2)}) collective-permute-start(bf16[64,256]{1,0:T(8,128)(2,1)S(1)} %collective-permute-done.8), channel_id=1, source_target_pairs={{0,2},{2,4},{4,6},{6,8},{8,10},{10,12},{12,14},{14,16},{16,18},{18... | collective-permute-start | bytes 98312 | tf_op jit(solution)/shard_map/ppermute | solution.py:71
  129.5 6.0 %collective-permute-start.10 = (bf16[64,256]{1,0:T(8,128)(2,1)S(1)}, bf16[64,256]{1,0:T(8,128)(2,1)S(1)}, u32[]{:S(2)}, u32[]{:S(2)}) collective-permute-start(bf16[64,256]{1,0:T(8,128)(2,1)S(1)} %collective-permute-done.9), channel_id=1, source_target_pairs={{0,2},{2,4},{4,6},{6,8},{8,10},{10,12},{12,14},{14,16},{16,18},{18... | collective-permute-start | bytes 98312 | tf_op jit(solution)/shard_map/ppermute | solution.py:71
  135.6 14.2 %collective-permute-start.11 = (bf16[64,256]{1,0:T(8,128)(2,1)S(1)}, bf16[64,256]{1,0:T(8,128)(2,1)S(1)}, u32[]{:S(2)}, u32[]{:S(2)}) collective-permute-start(bf16[64,256]{1,0:T(8,128)(2,1)S(1)} %collective-permute-done.10), channel_id=1, source_target_pairs={{0,2},{2,4},{4,6},{6,8},{8,10},{10,12},{12,14},{14,16},{16,18},{18... | collective-permute-start | bytes 98312 | tf_op jit(solution)/shard_map/ppermute | solution.py:71
  135.6 0.7 copy-start.5
  149.8 18.1 %collective-permute-start.12 = (bf16[64,256]{1,0:T(8,128)(2,1)S(1)}, bf16[64,256]{1,0:T(8,128)(2,1)S(1)}, u32[]{:S(2)}, u32[]{:S(2)}) collective-permute-start(bf16[64,256]{1,0:T(8,128)(2,1)S(1)} %collective-permute-done.11), channel_id=1, source_target_pairs={{0,2},{2,4},{4,6},{6,8},{8,10},{10,12},{12,14},{14,16},{16,18},{18... | collective-permute-start | bytes 98312 | tf_op jit(solution)/shard_map/ppermute | solution.py:71
  167.9 6.0 %collective-permute-start.13 = (bf16[64,256]{1,0:T(8,128)(2,1)S(1)}, bf16[64,256]{1,0:T(8,128)(2,1)S(1)}, u32[]{:S(2)}, u32[]{:S(2)}) collective-permute-start(bf16[64,256]{1,0:T(8,128)(2,1)S(1)} %collective-permute-done.12), channel_id=1, source_target_pairs={{0,2},{2,4},{4,6},{6,8},{8,10},{10,12},{12,14},{14,16},{16,18},{18... | collective-permute-start | bytes 98312 | tf_op jit(solution)/shard_map/ppermute | solution.py:71
  173.9 6.0 %collective-permute-start.14 = (bf16[64,256]{1,0:T(8,128)(2,1)S(1)}, bf16[64,256]{1,0:T(8,128)(2,1)S(1)}, u32[]{:S(2)}, u32[]{:S(2)}) collective-permute-start(bf16[64,256]{1,0:T(8,128)(2,1)S(1)} %collective-permute-done.13), channel_id=1, source_target_pairs={{0,2},{2,4},{4,6},{6,8},{8,10},{10,12},{12,14},{14,16},{16,18},{18... | collective-permute-start | bytes 98312 | tf_op jit(solution)/shard_map/ppermute | solution.py:71
  195.9 0.6 copy-start
Sparse Core Ops, SparseCore 0:
  196.6 18.2 all-reduce.2
